TPU v7x, 32 devices: a whole 2x2x4 slice. The times are simulated.
32 devices in a mesh: cx: 4 (over z), cy: 2 (over y), tp: 4 (over x, core).
Axes of the slice: x: 2, y: 2, z: 4, core: 2. Of those that a mesh axis runs over, the one named last changes fastest.
Arguments:
- neighbor_ids: int32 [16, 8, 128], P(('cx', 'cy'), 'tp'), may hold values from 0 to 1023
- decoder: bfloat16 [16, 64, 896], P(('cx', 'cy')), may hold values from -6 to 6
- table: bfloat16 [1024, 896], P(('cx', 'cy')), may hold values from -6 to 6
- attn_in: bfloat16 [6, 896, 896], P(None, ('cx', 'cy'), 'tp'), may hold values from -0.1875 to 0.1875
- attn_out: bfloat16 [2, 896, 896], P(None, 'tp', ('cx', 'cy')), may hold values from -0.1875 to 0.1875
- gains: float32 [3, 896], replicated, may hold values from 0.25 to 1.75
- w_up: bfloat16 [896, 3584], P(('cx', 'cy'), 'tp'), may hold values from -0.1875 to 0.1875
- w_down: bfloat16 [3584, 896], P('tp', ('cx', 'cy')), may hold values from -0.09375 to 0.09375
Outputs:
- encoded: bfloat16 [16, 8, 128, 896], P(('cx', 'cy'), 'tp')
All inputs are finite; a program needn't handle non-finite values.
Results may differ from a plain program's by a relative error of at most 0.013.
Values may be sent and summed in bfloat16 or wider, within the bound.
No kernel may reach another device: no remote copies, remote signals or barrier semaphores. Data moves between devices by JAX's collectives and lax.ppermute only.
A program may use at most 128 MiB of HBM per device.

v0:
```python
import jax
import jax.numpy as jnp
from jax import lax
from jax.sharding import PartitionSpec as P

HD = 64


def layer_norm(values, gain):
    middle = jnp.mean(values, axis=-1, keepdims=True)
    centred = values - middle
    spread = jnp.mean(centred * centred, axis=-1, keepdims=True)
    return (centred * lax.rsqrt(spread + 1e-05) * gain).astype(jnp.bfloat16)


def project(hidden, matrix):
    return jnp.dot(hidden, matrix, preferred_element_type=jnp.float32).astype(jnp.bfloat16)


def attend(query, key_rows, value_rows):
    batch, q_len, width = query.shape
    k_len = key_rows.shape[1]
    heads = width // HD
    q_heads = query.reshape(batch, q_len, heads, HD)
    k_heads = key_rows.reshape(batch, k_len, heads, HD)
    v_heads = value_rows.reshape(batch, k_len, heads, HD)
    scores = jnp.einsum(
        "bqhd,bkhd->bhqk", q_heads, k_heads, preferred_element_type=jnp.float32
    ) * HD ** (-0.5)
    probs = jax.nn.softmax(scores, axis=-1).astype(jnp.bfloat16)
    mixed = jnp.einsum("bhqk,bkhd->bqhd", probs, v_heads, preferred_element_type=jnp.float32)
    return mixed.reshape(batch, q_len, width).astype(jnp.bfloat16)


def body(neighbor_ids, decoder, table, attn_in, attn_out, gains, w_up, w_down):
    full_table, in_w, out_w, up_w, down_w = (
        lax.all_gather(table, ("cx", "cy"), axis=0, tiled=True),
        lax.all_gather(attn_in, ("cx", "cy"), axis=1, tiled=True),
        lax.all_gather(attn_out, ("cx", "cy"), axis=2, tiled=True),
        lax.all_gather(w_up, ("cx", "cy"), axis=0, tiled=True),
        lax.all_gather(w_down, ("cx", "cy"), axis=1, tiled=True),
    )
    spans, nbrs, length = neighbor_ids.shape
    width = full_table.shape[1]
    dec_len = decoder.shape[1]
    total = spans * nbrs * length
    dec_rows = decoder.reshape(spans * dec_len, width)
    x_zero = jnp.take(full_table, neighbor_ids.reshape(-1), axis=0).astype(jnp.float32)
    h_one = layer_norm(x_zero, gains[0])
    in_full, out_full = (
        lax.all_gather(in_w, "tp", axis=2, tiled=True),
        lax.all_gather(out_w, "tp", axis=1, tiled=True),
    )
    query = project(h_one, in_full[0]).reshape(spans * nbrs, length, width)
    keys = project(h_one, in_full[1]).reshape(spans * nbrs, length, width)
    values = project(h_one, in_full[2]).reshape(spans * nbrs, length, width)
    self_out = attend(query, keys, values).reshape(total, width)
    x_one = x_zero + jnp.dot(self_out, out_full[0], preferred_element_type=jnp.float32)
    h_two = layer_norm(x_one, gains[1])
    cross_q = project(h_two, in_full[3]).reshape(spans, nbrs * length, width)
    cross_k = project(dec_rows, in_full[4]).reshape(spans, dec_len, width)
    cross_v = project(dec_rows, in_full[5]).reshape(spans, dec_len, width)
    cross = attend(cross_q, cross_k, cross_v).reshape(total, width)
    x_two = x_one + jnp.dot(cross, out_full[1], preferred_element_type=jnp.float32)
    h_three = layer_norm(x_two, gains[2])
    every = lax.all_gather(h_three, "tp", axis=0, tiled=True)
    upward = jnp.dot(every, up_w, preferred_element_type=jnp.float32)
    act = jax.nn.gelu(upward, approximate=True).astype(jnp.bfloat16)
    mixed = lax.psum_scatter(
        jnp.dot(act, down_w, preferred_element_type=jnp.float32).astype(jnp.bfloat16),
        "tp",
        scatter_dimension=0,
        tiled=True,
    ).astype(jnp.float32)
    return (x_two + mixed).astype(jnp.bfloat16).reshape(spans, nbrs, length, width)


def solution(mesh):
    in_specs = (
        P(("cx", "cy"), "tp", None),
        P(("cx", "cy"), None, None),
        P(("cx", "cy"), None),
        P(None, ("cx", "cy"), "tp"),
        P(None, "tp", ("cx", "cy")),
        P(),
        P(("cx", "cy"), "tp"),
        P("tp", ("cx", "cy")),
    )
    out_specs = P(("cx", "cy"), "tp", None, None)
    return jax.shard_map(body, mesh=mesh, in_specs=in_specs, out_specs=out_specs, check_vma=False)
```

profile of v0, /device:TPU:0, one launch (start us, length us, event | category | flops | bytes accessed | tf_op | source)
XLA Modules:
  0.0 414.2 jit_solution(9565664598188071752)
XLA Ops:
  6.5 1.9 copy.66
  9.3 69.2 %all-gather.10.cloned.1.call-done = bf16[6,896,224]{2,0,1:T(8,128)(2,1)} async-done(((bf16[6,112,224]{2,0,1:T(8,128)(2,1)}), bf16[6,896,224]{2,0,1:T(8,128)(2,1)}) %all-gather.10.cloned.1.call-update) | async-done | bytes 2408464 | tf_op jit(solution)/shard_map/all_gather | solution.py:38
  78.5 6.1 %copy.67 = bf16[6,896,224]{1,2,0:T(8,128)(2,1)} copy(bf16[6,896,224]{2,0,1:T(8,128)(2,1)} %all-gather.10.cloned.1.call-done) | data formatting | bytes 4816896 | tf_op jit(solution)/shard_map/all_gather | solution.py:38
  85.6 34.5 %all_gather.27 = bf16[2,224,896]{1,0,2:T(2,128)(2,1)S(1)} all-gather(bf16[2,224,112]{1,0,2:T(2,128)(2,1)S(1)} %copy.76), channel_id=1, replica_groups=mesh['cx'=4,'cy'=2,'tp'=4] {'cx','cy'}, dimensions={2}, use_global_device_ids=true | all-gather | bytes 903168 | tf_op jit(solution)/shard_map/all_gather | solution.py:39
  120.1 2.2 copy.77
  123.7 7.4 %all-gather.8.cloned.1.call-done = bf16[1024,896]{1,0:T(8,128)(2,1)} async-done(((bf16[128,896]{1,0:T(8,128)(2,1)}), bf16[1024,896]{1,0:T(8,128)(2,1)}) %all-gather.8.cloned.1.call-update) | async-done | bytes 1835024 | tf_op jit(solution)/shard_map/all_gather | solution.py:37
  131.1 4.3 %gather_fusion = bf16[512,896]{1,0:T(8,128)(2,1)S(1)} fusion(bf16[1024,896]{1,0:T(8,128)(2,1)} %all-gather.8.cloned.1.call-done, s32[1024]{0:T(1024)S(1)} %pad_clamp_fusion), kind=kCustom, calls=%fused_computation | custom fusion | bytes 1837056 | tf_op jit(solution)/shard_map/jit(_take)/gather | solution.py:48
  136.2 61.5 %all-gather.12.cloned.1.call-done = bf16[6,896,896]{1,2,0:T(8,128)(2,1)} async-done(((bf16[6,896,224]{1,2,0:T(8,128)(2,1)}), bf16[6,896,896]{1,2,0:T(8,128)(2,1)}) %all-gather.12.cloned.1.call-update) | async-done | bytes 9633808 | tf_op jit(solution)/shard_map/all_gather | solution.py:51
  197.7 3.8 fusion.46
  201.5 2.9 reshape.106
  204.4 3.9 fusion.47
  208.3 4.0 reshape.107
  212.3 3.0 fusion.29
  215.3 2.7 fusion.82
  218.0 3.8 fusion.45
  221.7 3.1 reshape.105
  224.8 2.8 fusion.52
  228.4 2.8 fusion.83
  232.4 2.8 fusion.48
  235.1 1.4 reshape.109
  236.6 2.1 fusion.57
  239.0 2.7 fusion.56
  241.7 1.3 reshape.108
  243.8 1.2 copy-done.4
  245.5 2.2 fusion.55
  249.3 2.8 fusion.85
  253.7 21.0 %all-gather.18.cloned.1.call-done = bf16[896,896]{1,0:T(8,128)(2,1)} async-done(((bf16[112,896]{1,0:T(8,128)(2,1)}), bf16[896,896]{1,0:T(8,128)(2,1)}) %all-gather.18.cloned.1.call-update) | async-done | bytes 1605648 | tf_op jit(solution)/shard_map/all_gather | solution.py:40
  274.7 45.0 %all-gather.20.cloned.1.call-done = bf16[896,896]{0,1:T(8,128)(2,1)} async-done(((bf16[896,112]{0,1:T(8,128)(2,1)}), bf16[896,896]{0,1:T(8,128)(2,1)}) %all-gather.20.cloned.1.call-update) | async-done | bytes 1605648 | tf_op jit(solution)/shard_map/all_gather | solution.py:41
  319.7 31.4 %all-gather.16.cloned.1.call-done = bf16[2048,896]{1,0:T(8,128)(2,1)} async-done(((bf16[512,896]{1,0:T(8,128)(2,1)}), bf16[2048,896]{1,0:T(8,128)(2,1)}) %all-gather.16.cloned.1.call-update) | async-done | bytes 3670032 | tf_op jit(solution)/shard_map/all_gather | solution.py:66
  351.1 12.6 %fusion.16 = bf16[2048,896]{1,0:T(8,128)(2,1)} fusion(bf16[896,896]{0,1:T(8,128)(2,1)} %all-gather.20.cloned.1.call-done, bf16[2048,896]{1,0:T(8,128)(2,1)} %all-gather.16.cloned.1.call-done, bf16[896,896]{1,0:T(8,128)(2,1)} %all-gather.18.cloned.1.call-done), kind=kOutput, calls=%fused_computation.19 | convolution fusion | flops 6595018752 | bytes 10551296 | tf_op jit(solution)/shard_map/dot_general | solution.py:70
  363.7 41.4 %reduce-scatter.2.cloned.1.call-done = bf16[512,896]{1,0:T(8,128)(2,1)} async-done(((bf16[2048,896]{1,0:T(8,128)(2,1)}), bf16[512,896]{1,0:T(8,128)(2,1)}) %reduce-scatter.2.cloned.1.call-update) | async-done | bytes 917520 | tf_op jit(solution)/shard_map/reduce_scatter | solution.py:69
  405.1 2.3 add_convert_fusion
  (54 shorter events, 10.6 us)
Async XLA Ops:
  6.5 230.0 %copy-start = (bf16[2,64,896]{2,1,0:T(8,128)(2,1)S(1)}, bf16[2,64,896]{2,1,0:T(8,128)(2,1)}, u32[]{:S(2)}) copy-start(bf16[2,64,896]{2,1,0:T(8,128)(2,1)} %param.9) | copy-start | bytes 688132
  6.5 71.9 %all-gather.10.cloned.1.call-start = ((), (), s32[]{:S(2)}) async-start(), calls=%async_computation.2 | async-start | bytes 4128768 | tf_op jit(solution)/shard_map/all_gather | solution.py:38
  8.5 122.6 %all-gather.8.cloned.1.call-start = ((), (), s32[]{:S(2)}) async-start(), calls=%async_computation.1 | async-start | bytes 2064384 | tf_op jit(solution)/shard_map/all_gather | solution.py:37
  9.2 188.5 %all-gather.12.cloned.1.call-start = ((), (), s32[]{:S(2)}) async-start(), calls=%async_computation.3 | async-start | bytes 12042240 | tf_op jit(solution)/shard_map/all_gather | solution.py:51
  84.6 0.9 copy-start.5
  84.6 143.8 %all-gather.14.cloned.1.call-start = ((), (), s32[]{:S(2)}) async-start(), calls=%async_computation.4 | async-start | bytes 4014080 | tf_op jit(solution)/shard_map/all_gather | solution.py:52
  85.6 38.0 %copy-start.6 = (s32[2,2,128]{2,1,0:T(2,128)S(1)}, s32[2,2,128]{2,1,0:T(2,128)}, u32[]{:S(2)}) copy-start(s32[2,2,128]{2,1,0:T(2,128)} %param.8) | copy-start | bytes 6148
  85.6 38.0 %copy-start.7 = (f32[3,896]{1,0:T(4,128)S(1)}, f32[3,896]{1,0:T(4,128)}, u32[]{:S(2)}) copy-start(f32[3,896]{1,0:T(4,128)} %param.13) | copy-start | bytes 32260
  122.4 152.3 %all-gather.18.cloned.1.call-start = ((), (), s32[]{:S(2)}) async-start(), calls=%async_computation.6 | async-start | bytes 1806336 | tf_op jit(solution)/shard_map/all_gather | solution.py:40
  122.9 196.7 %all-gather.20.cloned.1.call-start = ((), (), s32[]{:S(2)}) async-start(), calls=%async_computation.7 | async-start | bytes 1806336 | tf_op jit(solution)/shard_map/all_gather | solution.py:41
  123.5 227.6 %all-gather.16.cloned.1.call-start = ((), (), s32[]{:S(2)}) async-start(), calls=%async_computation.5 | async-start | bytes 4587520 | tf_op jit(solution)/shard_map/all_gather | solution.py:66
  231.2 1.2 copy-start.2
  243.8 1.3 copy-start.4
  247.8 1.5 copy-start.3
  253.7 151.4 %reduce-scatter.2.cloned.1.call-start = ((), (), s32[]{:S(2)}) async-start(), calls=%async_computation.8 | async-start | bytes 4587520 | tf_op jit(solution)/shard_map/reduce_scatter | solution.py:69
  363.7 43.6 %copy-start.1 = (bf16[2,64,896]{2,1,0:T(8,128)(2,1)S(1)}, bf16[2,64,896]{2,1,0:T(8,128)(2,1)}, u32[]{:S(2)}) copy-start(bf16[2,64,896]{2,1,0:T(8,128)(2,1)} %param.9) | copy-start | bytes 688132
Sparse Core Ops, SparseCore 0:
  9.5 68.9 all-gather.9
  80.7 50.3 all-gather.7
  132.6 65.0 all-gather.11
  199.1 28.8 all-gather.13
  230.1 44.5 all-gather.17
  276.7 42.9 all-gather.19
  321.2 29.8 all-gather.15
  363.8 41.2 reduce-scatter.1
where the time goes:
time: 415 us; the launch traced here: 414 us
  waiting for transfers between devices  279 us (67%)
  matrix products  45.8 us (11%)
  blocking collectives  34.5 us (8%)
  local copies, waits for them, and re-layouts  32.9 us (8%)
  between operations  13.7 us (3%)
  other arithmetic  8.18 us (2%)
    all_gather x1, waiting for transfers between devices, body(): lax.all_gather(attn_in, ('cx', 'cy'), axis=1, tiled=True)  69.2 us
    all_gather x1, waiting for transfers between devices, body(): lax.all_gather(in_w, 'tp', axis=2, tiled=True)  61.5 us
    all_gather x1, waiting for transfers between devices, body(): lax.all_gather(w_down, ('cx', 'cy'), axis=1, tiled=True)  45 us
    reduce_scatter x1, waiting for transfers between devices, body(): lax.psum_scatter(jnp.dot(act, down_w, preferred_element_type=jnp.float32)...  41.4 us
    all_gather x1, blocking collectives, body(): lax.all_gather(attn_out, ('cx', 'cy'), axis=2, tiled=True)  34.5 us
    all_gather x1, waiting for transfers between devices, body(): every = lax.all_gather(h_three, 'tp', axis=0, tiled=True)  31.4 us
    all_gather x1, waiting for transfers between devices, body(): lax.all_gather(w_up, ('cx', 'cy'), axis=0, tiled=True)  21 us
    dot_general x6, matrix products, project(): jnp.dot(hidden, matrix, preferred_element_type=jnp.float32)  18.9 us
  transfers between devices with their start and end apart: 8, of which 7 were waited for; matrix products, arithmetic and copies ran while one was open for 16% of the time, Pallas kernels for 0%

commit v1 on v0

--- a/solution.py
+++ b/solution.py
@@ -63,7 +63,8 @@
     cross = attend(cross_q, cross_k, cross_v).reshape(total, width)
     x_two = x_one + jnp.dot(cross, out_full[1], preferred_element_type=jnp.float32)
     h_three = layer_norm(x_two, gains[2])
-    every = lax.all_gather(h_three, "tp", axis=0, tiled=True)
+    sent = jnp.stack([h_three] * lax.axis_size("tp"))
+    every = jnp.concatenate(lax.all_to_all(sent, "tp", 0, 0), axis=0)
     upward = jnp.dot(every, up_w, preferred_element_type=jnp.float32)
     act = jax.nn.gelu(upward, approximate=True).astype(jnp.bfloat16)
     mixed = lax.psum_scatter(

time: 415 us -> 382 us (0.920)
  waiting for transfers between devices: 279 us -> 241 us
  starting transfers between devices: 0.28 us -> 5.04 us
    all_gather x1 -> x0, waiting for transfers between devices: 31.4 us -> none  [body(): every = lax.all_gather(h_three, 'tp', axis=0, tiled=True)]
    all_to_all x0 -> x1, starting transfers between devices: none -> 4.8 us  [body(): every = jnp.concatenate(lax.all_to_all(sent, 'tp', 0, 0), axis=0)]
    all_gather x1, waiting for transfers between devices: 21 us -> 16.6 us  [body(): lax.all_gather(w_up, ('cx', 'cy'), axis=0, tiled=True)]
  transfers between devices with their start and end apart: 8 -> 8, of which waited for: 7 -> 6; matrix products, arithmetic and copies ran while one was open for 16% -> 17% of each run, Pallas kernels for 0% -> 0%
where the time goes in v1:
time: 382 us; the launch traced here: 381 us
  waiting for transfers between devices  241 us (63%)
  matrix products  45.1 us (12%)
  blocking collectives  34.5 us (9%)
  local copies, waits for them, and re-layouts  34.1 us (9%)
  between operations  13.8 us (4%)
  other arithmetic  7.26 us (2%)
  starting transfers between devices  5.04 us (1%)
    all_gather x1, waiting for transfers between devices, body(): lax.all_gather(attn_in, ('cx', 'cy'), axis=1, tiled=True)  69.2 us
    all_gather x1, waiting for transfers between devices, body(): lax.all_gather(in_w, 'tp', axis=2, tiled=True)  61.5 us
    all_gather x1, waiting for transfers between devices, body(): lax.all_gather(w_down, ('cx', 'cy'), axis=1, tiled=True)  44.9 us
    reduce_scatter x1, waiting for transfers between devices, body(): lax.psum_scatter(jnp.dot(act, down_w, preferred_element_type=jnp.float32)...  39.7 us
    all_gather x1, blocking collectives, body(): lax.all_gather(attn_out, ('cx', 'cy'), axis=2, tiled=True)  34.5 us
    dot_general x6, matrix products, project(): jnp.dot(hidden, matrix, preferred_element_type=jnp.float32)  18.2 us
    all_gather x1, waiting for transfers between devices, body(): lax.all_gather(w_up, ('cx', 'cy'), axis=0, tiled=True)  16.6 us
    dot_general x1, matrix products, body(): jnp.dot(act, down_w, preferred_element_type=jnp.float32)  12.6 us
  transfers between devices with their start and end apart: 8, of which 6 were waited for; matrix products, arithmetic and copies ran while one was open for 17% of the time, Pallas kernels for 0%

profile of v1, /device:TPU:0, one launch (start us, length us, event | category | flops | bytes accessed | tf_op | source)
XLA Modules:
  0.0 381.0 jit_solution(6120966384473412586)
XLA Ops:
  6.5 1.9 copy.66
  9.3 69.2 %all-gather.9.cloned.1.call-done = bf16[6,896,224]{2,0,1:T(8,128)(2,1)} async-done(((bf16[6,112,224]{2,0,1:T(8,128)(2,1)}), bf16[6,896,224]{2,0,1:T(8,128)(2,1)}) %all-gather.9.cloned.1.call-update) | async-done | bytes 2408464 | tf_op jit(solution)/shard_map/all_gather | solution.py:38
  78.5 6.1 %copy.67 = bf16[6,896,224]{1,2,0:T(8,128)(2,1)} copy(bf16[6,896,224]{2,0,1:T(8,128)(2,1)} %all-gather.9.cloned.1.call-done) | data formatting | bytes 4816896 | tf_op jit(solution)/shard_map/all_gather | solution.py:38
  85.6 34.5 %all_gather.24 = bf16[2,224,896]{1,0,2:T(2,128)(2,1)S(1)} all-gather(bf16[2,224,112]{1,0,2:T(2,128)(2,1)S(1)} %copy.76), channel_id=1, replica_groups=mesh['cx'=4,'cy'=2,'tp'=4] {'cx','cy'}, dimensions={2}, use_global_device_ids=true | all-gather | bytes 903168 | tf_op jit(solution)/shard_map/all_gather | solution.py:39
  120.1 2.2 copy.77
  123.6 7.5 %all-gather.7.cloned.1.call-done = bf16[1024,896]{1,0:T(8,128)(2,1)} async-done(((bf16[128,896]{1,0:T(8,128)(2,1)}), bf16[1024,896]{1,0:T(8,128)(2,1)}) %all-gather.7.cloned.1.call-update) | async-done | bytes 1835024 | tf_op jit(solution)/shard_map/all_gather | solution.py:37
  131.1 4.3 %gather_fusion = bf16[512,896]{1,0:T(8,128)(2,1)S(1)} fusion(bf16[1024,896]{1,0:T(8,128)(2,1)} %all-gather.7.cloned.1.call-done, s32[1024]{0:T(1024)S(1)} %pad_clamp_fusion), kind=kCustom, calls=%fused_computation | custom fusion | bytes 1837056 | tf_op jit(solution)/shard_map/jit(_take)/gather | solution.py:48
  136.2 61.5 %all-gather.11.cloned.1.call-done = bf16[6,896,896]{1,2,0:T(8,128)(2,1)} async-done(((bf16[6,896,224]{1,2,0:T(8,128)(2,1)}), bf16[6,896,896]{1,2,0:T(8,128)(2,1)}) %all-gather.11.cloned.1.call-update) | async-done | bytes 9633808 | tf_op jit(solution)/shard_map/all_gather | solution.py:51
  197.7 3.8 fusion.46
  201.5 2.9 reshape.112
  204.4 3.9 %fusion.47 = bf16[512,896]{1,0:T(8,128)(2,1)} fusion(bf16[6,896,896]{1,2,0:T(8,128)(2,1)} %all-gather.11.cloned.1.call-done, f32[896]{0:T(1024)S(1)} %get-tuple-element.6, f32[512]{0:T(512)S(1)} %add_rsqrt_fusion.2, f32[512]{0:T(512)S(1)} %broadcast_multiply_fusion.2, bf16[512,896]{1,0:T(8,128)(2,1)S(1)} %gather_fusion, pred[512]{0:T(512)(128)(4,1)S(1)} %compare_and_fusion), kind=kOutput, calls=%fused_computation.66 | convolution fusion | flops 825294848 | bytes 3448832 | tf_op jit(solution)/shard_map/dot_general | solution.py:17
  208.3 4.0 %reshape.113 = bf16[4,128,14,64]{3,2,1,0:T(8,128)(2,1)} reshape(bf16[512,896]{1,0:T(8,128)(2,1)} %fusion.47) | data formatting | bytes 1835008 | tf_op jit(solution)/shard_map/reshape;reshape | solution.py:25
  212.3 3.0 fusion.29
  215.3 2.7 fusion.82
  218.0 3.8 fusion.45
  221.7 3.1 reshape.111
  224.8 2.8 fusion.52
  228.4 2.8 fusion.83
  232.4 2.8 fusion.48
  235.1 1.4 reshape.115
  236.6 2.1 fusion.57
  239.8 1.2 copy-done.4
  241.5 2.0 fusion.56
  243.9 2.2 fusion.55
  247.7 2.8 fusion.85
  251.1 2.1 stack.2
  253.3 4.8 %all-to-all-start = ((bf16[4,512,896]{2,1,0:T(8,128)(2,1)}), bf16[4,512,896]{2,1,0:T(8,128)(2,1)}, u32[]{:S(2)}, u32[]{:S(2)}) async-start(bf16[4,512,896]{2,1,0:T(8,128)(2,1)} %stack.2), calls=%async_computation | async-start | bytes 7340032 | tf_op jit(solution)/shard_map/all_to_all | solution.py:67
  258.1 16.6 %all-gather.15.cloned.1.call-done = bf16[896,896]{1,0:T(8,128)(2,1)} async-done(((bf16[112,896]{1,0:T(8,128)(2,1)}), bf16[896,896]{1,0:T(8,128)(2,1)}) %all-gather.15.cloned.1.call-update) | async-done | bytes 1605648 | tf_op jit(solution)/shard_map/all_gather | solution.py:40
  274.7 44.9 %all-gather.17.cloned.1.call-done = bf16[896,896]{0,1:T(8,128)(2,1)} async-done(((bf16[896,112]{0,1:T(8,128)(2,1)}), bf16[896,896]{0,1:T(8,128)(2,1)}) %all-gather.17.cloned.1.call-update) | async-done | bytes 1605648 | tf_op jit(solution)/shard_map/all_gather | solution.py:41
  319.6 12.6 %fusion.16 = bf16[2048,896]{1,0:T(8,128)(2,1)} fusion(bf16[896,896]{0,1:T(8,128)(2,1)} %all-gather.17.cloned.1.call-done, bf16[2048,896]{1,0:T(8,128)(2,1)} %bitcast.14, bf16[896,896]{1,0:T(8,128)(2,1)} %all-gather.15.cloned.1.call-done), kind=kOutput, calls=%fused_computation.19 | convolution fusion | flops 6595018752 | bytes 10551296 | tf_op jit(solution)/shard_map/dot_general | solution.py:71
  332.2 39.7 %reduce-scatter.2.cloned.1.call-done = bf16[512,896]{1,0:T(8,128)(2,1)} async-done(((bf16[2048,896]{1,0:T(8,128)(2,1)}), bf16[512,896]{1,0:T(8,128)(2,1)}) %reduce-scatter.2.cloned.1.call-update) | async-done | bytes 917520 | tf_op jit(solution)/shard_map/reduce_scatter | solution.py:70
  371.9 2.3 add_convert_fusion
  (54 shorter events, 10.0 us)
Async XLA Ops:
  6.5 230.0 %copy-start = (bf16[2,64,896]{2,1,0:T(8,128)(2,1)S(1)}, bf16[2,64,896]{2,1,0:T(8,128)(2,1)}, u32[]{:S(2)}) copy-start(bf16[2,64,896]{2,1,0:T(8,128)(2,1)} %param.9) | copy-start | bytes 688132
  6.5 71.9 %all-gather.9.cloned.1.call-start = ((), (), s32[]{:S(2)}) async-start(), calls=%async_computation.3 | async-start | bytes 4128768 | tf_op jit(solution)/shard_map/all_gather | solution.py:38
  8.5 122.6 %all-gather.7.cloned.1.call-start = ((), (), s32[]{:S(2)}) async-start(), calls=%async_computation.2 | async-start | bytes 2064384 | tf_op jit(solution)/shard_map/all_gather | solution.py:37
  9.2 188.5 %all-gather.11.cloned.1.call-start = ((), (), s32[]{:S(2)}) async-start(), calls=%async_computation.4 | async-start | bytes 12042240 | tf_op jit(solution)/shard_map/all_gather | solution.py:51
  84.6 0.9 copy-start.5
  84.6 143.8 %all-gather.13.cloned.1.call-start = ((), (), s32[]{:S(2)}) async-start(), calls=%async_computation.5 | async-start | bytes 4014080 | tf_op jit(solution)/shard_map/all_gather | solution.py:52
  85.6 37.9 %copy-start.6 = (s32[2,2,128]{2,1,0:T(2,128)S(1)}, s32[2,2,128]{2,1,0:T(2,128)}, u32[]{:S(2)}) copy-start(s32[2,2,128]{2,1,0:T(2,128)} %param.8) | copy-start | bytes 6148
  85.6 38.0 %copy-start.7 = (f32[3,896]{1,0:T(4,128)S(1)}, f32[3,896]{1,0:T(4,128)}, u32[]{:S(2)}) copy-start(f32[3,896]{1,0:T(4,128)} %param.13) | copy-start | bytes 32260
  122.4 152.3 %all-gather.15.cloned.1.call-start = ((), (), s32[]{:S(2)}) async-start(), calls=%async_computation.6 | async-start | bytes 1806336 | tf_op jit(solution)/shard_map/all_gather | solution.py:40
  122.9 196.6 %all-gather.17.cloned.1.call-start = ((), (), s32[]{:S(2)}) async-start(), calls=%async_computation.7 | async-start | bytes 1806336 | tf_op jit(solution)/shard_map/all_gather | solution.py:41
  231.2 1.2 copy-start.2
  239.8 1.2 copy-start.4
  246.2 1.5 copy-start.3
  253.3 66.3 %all-to-all-start = ((bf16[4,512,896]{2,1,0:T(8,128)(2,1)}), bf16[4,512,896]{2,1,0:T(8,128)(2,1)}, u32[]{:S(2)}, u32[]{:S(2)}) async-start(bf16[4,512,896]{2,1,0:T(8,128)(2,1)} %stack.2), calls=%async_computation | async-start | bytes 7340032 | tf_op jit(solution)/shard_map/all_to_all | solution.py:67
  258.1 113.9 %reduce-scatter.2.cloned.1.call-start = ((), (), s32[]{:S(2)}) async-start(), calls=%async_computation.8 | async-start | bytes 4587520 | tf_op jit(solution)/shard_map/reduce_scatter | solution.py:70
  332.2 42.0 %copy-start.1 = (bf16[2,64,896]{2,1,0:T(8,128)(2,1)S(1)}, bf16[2,64,896]{2,1,0:T(8,128)(2,1)}, u32[]{:S(2)}) copy-start(bf16[2,64,896]{2,1,0:T(8,128)(2,1)} %param.9) | copy-start | bytes 688132
Sparse Core Ops, SparseCore 0:
  9.5 68.9 all-gather.8
  80.7 50.3 all-gather.6
  132.6 65.0 all-gather.10
  199.1 28.8 all-gather.12
  230.1 44.5 all-gather.14
  276.7 42.8 all-gather.16
  332.3 39.5 reduce-scatter.1
